TPU v7x, 32 devices: a whole 2x2x4 slice. The times are simulated.
32 devices in a mesh: row: 2 (over y), theta: 4 (over x, core), gz: 4 (over z).
Axes of the slice: x: 2, y: 2, z: 4, core: 2. Of those that a mesh axis runs over, the one named last changes fastest.
Arguments:
- state_start: float32 [6, 8, 128, 1024], P(None, 'row', 'gz', 'theta'), may hold values from -1.2 to 1.2
- state_section: float32 [6, 8, 128, 1024], P(None, 'row', 'gz', 'theta'), may hold values from -1.5 to 4, as said below
- phase: int32 [8, 128, 1024], P('row', 'gz', 'theta'), may hold values 0 or 1
- cutoff: int32 [4], replicated, may hold values from 1 to 63
Outputs:
- state_next: float32 [6, 8, 128, 1024], P(None, 'row', 'gz', 'theta')
Inputs may be any that keep to these rules, and one draw needn't show every extreme that they name: `state_section`: channel 0 (density) lies in 0.5 to 2.0, channels 1 to 3 (momenta) in -1.5 to 1.5, channel 4 (total energy) in 2.5 to 4.0, channel 5 (jet mass density) in 0 to 1.0.
All inputs are finite; a program needn't handle non-finite values. No bound on the sum of `phase` on one device may be relied on, other than what follows from the above.
Results may differ from a plain program's by a relative error of at most 0.0003.
Values sent between devices are 32-bit elements; how exact they have to be, the bound alone decides.
A program may use at most 64 MiB of HBM per device.

v0:
```python
import math
import jax
import jax.numpy as jnp
from jax import lax
from jax.sharding import PartitionSpec as P

NT = 1024
KMODES = 64
split_speed = 10.0
time_step = 0.05
weno_epsilon = 1e-06
liquid_ratio = 4.4
gas_ratio = 1.4
liquid_stiffness = 0.6


def passed_along(value, axis, steps):
    count = lax.axis_size(axis)
    pairs = [(source, (source + steps) % count) for source in range(count)]
    return lax.ppermute(value, axis, pairs)


def with_halo(cells, sides, width):
    for axis, dim in sides:
        count = lax.axis_size(axis)
        head = lax.slice_in_dim(cells, 0, width, axis=dim)
        tail = lax.slice_in_dim(cells, cells.shape[dim] - width, cells.shape[dim], axis=dim)
        cells = jnp.concatenate(
            [
                lax.ppermute(tail, axis, [(i, (i + 1) % count) for i in range(count)]),
                cells,
                lax.ppermute(head, axis, [((i + 1) % count, i) for i in range(count)]),
            ],
            axis=dim,
        )
    return cells


def pressure_of(state, phase):
    density = state[0]
    kinetic = 0.5 * (state[1] * state[1] + state[2] * state[2] + state[3] * state[3]) / density
    liquid = phase == 1
    heat_ratio = jnp.where(liquid, liquid_ratio, gas_ratio)
    stiffness = jnp.where(liquid, liquid_stiffness, 0.0)
    return (heat_ratio - 1.0) * (state[4] - kinetic) - heat_ratio * stiffness


def weno_face(far_left, near_left, centre, near_right, far_right):
    smooth_left = (
        13.0 / 12.0 * (far_left - 2.0 * near_left + centre) ** 2
        + 0.25 * (far_left - 4.0 * near_left + 3.0 * centre) ** 2
    )
    smooth_mid = (
        13.0 / 12.0 * (near_left - 2.0 * centre + near_right) ** 2
        + 0.25 * (near_left - near_right) ** 2
    )
    smooth_right = (
        13.0 / 12.0 * (centre - 2.0 * near_right + far_right) ** 2
        + 0.25 * (3.0 * centre - 4.0 * near_right + far_right) ** 2
    )
    weight_left = 0.1 / (weno_epsilon + smooth_left) ** 2
    weight_mid = 0.6 / (weno_epsilon + smooth_mid) ** 2
    weight_right = 0.3 / (weno_epsilon + smooth_right) ** 2
    weight_sum = weight_left + weight_mid + weight_right
    value_left = (2.0 * far_left - 7.0 * near_left + 11.0 * centre) / 6.0
    value_mid = (-near_left + 5.0 * centre + 2.0 * near_right) / 6.0
    value_right = (2.0 * centre + 5.0 * near_right - far_right) / 6.0
    return (
        weight_left * value_left + weight_mid * value_mid + weight_right * value_right
    ) / weight_sum


def face_fluxes(padded_line, array_axis, component):
    density = padded_line[0]
    velocity = padded_line[component] / density
    pressure_field = padded_line[6]
    conserved = padded_line[:6]
    flux_rows = [conserved[channel] * velocity for channel in range(6)]
    flux_rows[component] = flux_rows[component] + pressure_field
    flux_rows[4] = flux_rows[4] + pressure_field * velocity
    physical = jnp.stack(flux_rows)
    upward = 0.5 * (physical + split_speed * conserved)
    downward = 0.5 * (physical - split_speed * conserved)
    face_count = padded_line.shape[array_axis] - 5

    def shifted(values, offset):
        return lax.slice_in_dim(values, offset, offset + face_count, axis=array_axis)

    upwind_part = weno_face(
        shifted(upward, 0),
        shifted(upward, 1),
        shifted(upward, 2),
        shifted(upward, 3),
        shifted(upward, 4),
    )
    downwind_part = weno_face(
        shifted(downward, 5),
        shifted(downward, 4),
        shifted(downward, 3),
        shifted(downward, 2),
        shifted(downward, 1),
    )
    return upwind_part + downwind_part


def tendency(centre_cells, radial_line, axial_line, azimuth_line, cycle_start):
    cycle_count = centre_cells.shape[1]
    radial_flux = face_fluxes(radial_line, 1, 1)
    axial_flux = face_fluxes(axial_line, 2, 3)
    azimuth_flux = face_fluxes(azimuth_line, 3, 2)
    cycle_index = (cycle_start + lax.iota(jnp.int32, cycle_count + 1)).astype(centre_cells.dtype)
    face_radius = cycle_index[None, :, None, None]
    cell_radius = face_radius[:, :-1] + 0.5
    weighted = face_radius * radial_flux
    div_radial = (weighted[:, 1:] - weighted[:, :-1]) / cell_radius
    div_axial = axial_flux[:, :, 1:] - axial_flux[:, :, :-1]
    angle_step = 2.0 * math.pi / NT
    div_azimuth = (azimuth_flux[..., 1:] - azimuth_flux[..., :-1]) / (cell_radius * angle_step)
    density = centre_cells[0]
    swirl_speed = centre_cells[2] / density
    radius = cell_radius[0]
    source_radial = (centre_cells[2] * swirl_speed + centre_cells[6]) / radius
    source_swirl = -centre_cells[1] * swirl_speed / radius
    zero_field = jnp.zeros_like(density)
    source = jnp.stack(
        [zero_field, source_radial, source_swirl, zero_field, zero_field, zero_field]
    )
    return source - div_radial - div_axial - div_azimuth


def across_axis(partner):
    sign_flip = jnp.array([1.0, -1.0, -1.0, 1.0, 1.0, 1.0, 1.0], partner.dtype)[:, None, None, None]
    return partner[:, ::-1] * sign_flip


def build_table(positions, mode_count, length):
    orders = lax.iota(jnp.int32, mode_count)
    phases = positions[:, None] * orders[None, :] % length
    angles = phases.astype(jnp.float32) * (2.0 * math.pi / length)
    return jnp.concatenate([jnp.cos(angles), jnp.sin(angles)], 1)


def cycle_weights(cutoff, mode_count, length):
    orders = lax.iota(jnp.int32, mode_count)
    mode_scale = jnp.where(orders == 0, 1.0 / length, 2.0 / length)
    kept_modes = orders[None, :] <= cutoff[:, None]
    weight_half = jnp.where(kept_modes, mode_scale[None, :], 0.0)
    return jnp.concatenate([weight_half, weight_half], 1)


def apply_filter(cycle_block, weights, theta_id):
    local_theta = cycle_block.shape[3]
    positions = theta_id * local_theta + lax.iota(jnp.int32, local_theta)
    fourier_table = build_table(positions, KMODES, NT)
    coefficients = jnp.einsum(
        "vizt,tk->vizk", cycle_block, fourier_table, precision=lax.Precision.HIGHEST
    )
    coefficients = lax.psum(coefficients, "theta")
    coefficients = coefficients * weights[None, :, None, :]
    return jnp.einsum("vizk,tk->vizt", coefficients, fourier_table, precision=lax.Precision.HIGHEST)


def shards(state_start, state_section, phase, cutoff):
    row_count = lax.axis_size("row")
    row_id = lax.axis_index("row")
    theta_count = lax.axis_size("theta")
    theta_id = lax.axis_index("theta")
    cycle_count = state_section.shape[1]
    filtered_count = cutoff.shape[0]
    pressure_field = pressure_of(state_section, phase)
    fields = jnp.concatenate([state_section, pressure_field[None]], 0)
    partner = passed_along(fields[:, 0:3], "theta", theta_count // 2)
    mirror = across_axis(partner)
    outer_rim = jnp.repeat(fields[:, -1:], 3, axis=1)
    padded = with_halo(fields, (("row", 1), ("theta", 3), ("gz", 2)), 3)
    radial_line = padded[:, :, 3:-3, 3:-3]
    axial_line = padded[:, 3:-3, :, 3:-3]
    azimuth_line = padded[:, 3:-3, 3:-3, :]
    lower_rim = jnp.where(row_id == 0, mirror, radial_line[:, :3])
    upper_rim = jnp.where(row_id == row_count - 1, outer_rim, radial_line[:, -3:])
    radial_line = jnp.concatenate([lower_rim, fields, upper_rim], 1)
    tendencies = tendency(fields, radial_line, axial_line, azimuth_line, row_id * cycle_count)
    advanced = 0.75 * state_start + 0.25 * (state_section + time_step * tendencies)
    weights = cycle_weights(cutoff, KMODES, NT)
    filtered = apply_filter(advanced, weights, theta_id)
    inner_next = jnp.where(row_id == 0, filtered, advanced)
    return jnp.concatenate([inner_next, advanced[:, filtered_count:]], 1)


def solution(mesh):
    in_specs = (
        P(None, "row", "gz", "theta"),
        P(None, "row", "gz", "theta"),
        P("row", "gz", "theta"),
        P(),
    )
    out_specs = P(None, "row", "gz", "theta")
    return jax.shard_map(shards, mesh=mesh, in_specs=in_specs, out_specs=out_specs, check_vma=False)
```

profile of v0, /device:TPU:0, one launch (start us, length us, event | category | flops | bytes accessed | tf_op | source)
XLA Modules:
  0.0 148.2 jit_solution(16903499594754744437)
XLA Ops:
  6.6 1.4 bitcast_dynamic-update-slice_fusion
  8.0 1.2 fusion.11
  9.2 3.0 %collective-permute-start.2 = (f32[7,3,32,256]{3,2,1,0:T(8,128)}, f32[7,3,32,256]{3,2,1,0:T(8,128)S(1)}, u32[]{:S(2)}, u32[]{:S(2)}) collective-permute-start(f32[7,3,32,256]{3,2,1,0:T(8,128)} %get-tuple-element.24), channel_id=1, source_target_pairs={{16,0},{0,16},{17,1},{1,17},{18,2},{2,18},{19,3},{3,19},{20,4},{4,... | collective-permute-start | bytes 2064392 | tf_op jit(solution)/shard_map/ppermute | solution.py:32
  12.2 1.5 %collective-permute-start = (f32[7,3,32,256]{3,2,1,0:T(8,128)}, f32[7,3,32,256]{3,2,1,0:T(8,128)}, u32[]{:S(2)}, u32[]{:S(2)}) collective-permute-start(f32[7,3,32,256]{3,2,1,0:T(8,128)} %get-tuple-element.24), channel_id=1, source_target_pairs={{0,8},{4,12},{8,0},{12,4},{1,9},{5,13},{9,1},{13,5},{2,10},{6,14},... | collective-permute-start | bytes 2064392 | tf_op jit(solution)/shard_map/ppermute | solution.py:20
  13.7 0.5 collective-permute-start.1
  14.2 0.1 divide_dynamic-update-slice_fusion
  14.5 0.6 fusion.47
  15.1 13.7 %collective-permute-done.2 = f32[7,3,32,256]{3,2,1,0:T(8,128)S(1)} collective-permute-done((f32[7,3,32,256]{3,2,1,0:T(8,128)}, f32[7,3,32,256]{3,2,1,0:T(8,128)S(1)}, u32[]{:S(2)}, u32[]{:S(2)}) %collective-permute-start.2) | collective-permute-done | bytes 688160 | tf_op jit(solution)/shard_map/ppermute | solution.py:32
  28.8 13.8 %collective-permute-done.1 = f32[7,3,32,256]{3,2,1,0:T(8,128)S(1)} collective-permute-done((f32[7,3,32,256]{3,2,1,0:T(8,128)}, f32[7,3,32,256]{3,2,1,0:T(8,128)S(1)}, u32[]{:S(2)}, u32[]{:S(2)}) %collective-permute-start.1) | collective-permute-done | bytes 688160 | tf_op jit(solution)/shard_map/ppermute | solution.py:30
  42.6 1.5 %multiply_select_fusion = f32[7,3,32,256]{3,2,1,0:T(8,128)S(1)} fusion(f32[7,3,32,256]{3,2,1,0:T(8,128)S(1)} %collective-permute-done.1, f32[7,3,32,256]{3,2,1,0:T(8,128)} %collective-permute-done, f32[7]{0:T(128)S(1)} %copy-done.10, pred[]{:T(512)S(6)} %eq.25), kind=kLoop, calls=%fused_computation.37 | loop fusion | flops 344064 | bytes 2064413 | tf_op jit(solution)/shard_map/jit(_where)/select_n | solution.py:179
  44.2 1.9 %pad_maximum_fusion.2 = (f32[7,10,32,256]{3,2,1,0:T(8,128)}, f32[7,10,32,256]{3,2,1,0:T(8,128)S(1)}) fusion(f32[7,3,32,256]{3,2,1,0:T(8,128)S(1)} %broadcast_select_fusion, f32[1,4,32,256]{3,2,1,0:T(8,128)S(1)} %bitcast.49, f32[6,4,32,256]{3,2,1,0:T(8,128)S(1)} %copy-done, f32[7,3,32,256]{3,2,1,0:T(8,128)S(1)} %multiply_select_fusion, ...), kind=kLoop, calls=%fused_computation.2 | loop fusion | flops 2867200 | bytes 8257536 | tf_op jit(solution)/shard_map/concatenate | solution.py:181
  46.1 1.8 %fusion.56 = (f32[7,10,32,3]{3,2,1,0:T(8,128)}, f32[7,10,32,3]{3,2,1,0:T(8,128)}) fusion(f32[7,10,32,256]{3,2,1,0:T(8,128)S(1)} %get-tuple-element.22), kind=kLoop, calls=%fused_computation.127 | loop fusion | bytes 107520 | tf_op jit(solution)/shard_map/slice | solution.py:27
  47.9 2.6 %copy.7 = f32[7,10,32,3]{2,0,3,1:T(8,128)} copy(f32[7,10,32,3]{3,2,1,0:T(8,128)} %get-tuple-element.20) | data formatting | bytes 53760 | tf_op jit(solution)/shard_map/slice | solution.py:26
  50.5 0.3 collective-permute-start.4
  50.8 2.4 %copy.6 = f32[7,10,32,3]{2,0,3,1:T(8,128)} copy(f32[7,10,32,3]{3,2,1,0:T(8,128)} %get-tuple-element.19) | data formatting | bytes 53760 | tf_op jit(solution)/shard_map/slice | solution.py:27
  53.2 0.2 collective-permute-start.3
  53.8 0.7 add_multiply_fusion
  54.5 5.2 %add_multiply_fusion.3 = f32[6,5,32,256]{3,2,1,0:T(8,128)} fusion(f32[6,10,32,256]{3,2,1,0:T(8,128)S(1)} %get-tuple-element.16, f32[6,10,32,256]{3,2,1,0:T(8,128)S(1)} %get-tuple-element.15, f32[5]{0:T(128)S(1)} %add_convert_fusion), kind=kLoop, calls=%fused_computation.20 | loop fusion | flops 31948800 | bytes 10813460 | tf_op jit(solution)/shard_map/mul | solution.py:114
  59.7 1.4 copy.9
  61.1 1.4 copy.8
  62.5 2.6 %pad_maximum_fusion.1 = f32[7,10,32,262]{3,2,1,0:T(8,128)S(1)} fusion(f32[7,10,32,3]{3,2,1,0:T(8,128)S(1)} %copy.9, f32[7,3,32,256]{3,2,1,0:T(8,128)} %copy-done.3, f32[1,4,32,256]{3,2,1,0:T(8,128)S(1)} %bitcast.50, f32[6,4,32,256]{3,2,1,0:T(8,128)S(1)} %copy-done, f32[7,3,32,256]{3,2,1,0:T(8,128)} %copy-done.1, f32[7,10,32,3]{3,2,1,0:T(8,128)S(1)} %copy.8), kind=kLoop, calls=%fused_computation.1 | loop fusion | flops 2934400 | bytes 4695040 | tf_op jit(solution)/shard_map/concatenate | solution.py:28
  65.1 0.2 fusion.55
  65.2 0.9 copy-done.2
  66.1 0.2 copy-done.4
  66.4 0.2 multiply_dynamic-update-slice_fusion.1
  66.6 0.3 fusion.26
  66.8 0.3 fusion.25
  67.1 0.3 fusion.23
  67.4 0.3 fusion.22
  67.7 0.3 fusion.20
  68.0 0.3 add_multiply_fusion.1
  68.3 3.9 %collective-permute-start.6 = (f32[7,10,3,262]{3,2,1,0:T(4,128)S(1)}, f32[7,10,3,262]{3,2,1,0:T(4,128)S(1)}, u32[]{:S(2)}, u32[]{:S(2)}) collective-permute-start(f32[7,10,3,262]{3,2,1,0:T(4,128)S(1)} %get-tuple-element.18), channel_id=1, source_target_pairs={{1,0},{2,1},{3,2},{0,3},{5,4},{6,5},{7,6},{4,7},{9,8},{10,9},{11,1... | collective-permute-start | bytes 660248 | tf_op jit(solution)/shard_map/ppermute | solution.py:32
  72.2 5.9 %divide_add_fusion = f32[6,4,32,257]{3,2,1,0:T(8,128)S(1)} fusion(f32[6,4,32,262]{3,2,1,0:T(8,128)S(1)} %get-tuple-element.14, f32[6,4,32,262]{3,2,1,0:T(8,128)S(1)} %get-tuple-element.13), kind=kLoop, calls=%fused_computation.13 | loop fusion | flops 25461504 | bytes 8684544 | tf_op jit(solution)/shard_map/add | solution.py:103
  78.1 4.3 %collective-permute-done.6 = f32[7,10,3,262]{3,2,1,0:T(4,128)S(1)} collective-permute-done((f32[7,10,3,262]{3,2,1,0:T(4,128)S(1)}, f32[7,10,3,262]{3,2,1,0:T(4,128)S(1)}, u32[]{:S(2)}, u32[]{:S(2)}) %collective-permute-start.6) | collective-permute-done | bytes 220112 | tf_op jit(solution)/shard_map/ppermute | solution.py:32
  82.4 10.1 %collective-permute-done.5 = f32[7,10,3,262]{3,2,1,0:T(4,128)S(1)} collective-permute-done((f32[7,10,3,262]{3,2,1,0:T(4,128)S(1)}, f32[7,10,3,262]{3,2,1,0:T(4,128)S(1)}, u32[]{:S(2)}, u32[]{:S(2)}) %collective-permute-start.5) | collective-permute-done | bytes 220112 | tf_op jit(solution)/shard_map/ppermute | solution.py:30
  92.5 5.7 %pad_maximum_fusion = f32[7,10,38,262]{3,2,1,0:T(8,128)S(1)} fusion(f32[7,10,3,262]{3,2,1,0:T(4,128)S(1)} %collective-permute-done.6, f32[7,10,32,3]{3,2,1,0:T(8,128)S(1)} %copy.9, f32[7,3,32,256]{3,2,1,0:T(8,128)S(1)} %copy-done.4, f32[1,4,32,256]{3,2,1,0:T(8,128)S(1)} %bitcast.57, f32[6,4,32,256]{3,2,1,0:T(8,128)S(1)} %copy-done, ...), kind=kLoop, calls=%fused_computation | loop fusion | flops 4878440 | bytes 5575360 | tf_op jit(solution)/shard_map/concatenate | solution.py:28
  98.2 0.2 multiply_dynamic-update-slice_fusion.2
  98.4 0.1 fusion.32
  98.5 0.1 fusion.31
  98.6 0.2 add_dynamic-update-slice_fusion.1
  98.8 0.2 fusion.30
  98.9 0.1 fusion.28
  99.1 0.3 add_multiply_fusion.2
  99.4 5.0 %divide_add_fusion.1 = f32[6,4,33,256]{3,2,1,0:T(8,128)S(1)} fusion(f32[6,4,38,256]{3,2,1,0:T(8,128)S(1)} %get-tuple-element.12, f32[6,4,38,256]{3,2,1,0:T(8,128)S(1)} %get-tuple-element.11), kind=kLoop, calls=%fused_computation.17 | loop fusion | flops 26155008 | bytes 8921088 | tf_op jit(solution)/shard_map/add | solution.py:103
  104.5 0.7 fusion.7
  105.2 1.6 %fusion.48 = f32[6,4,32,128]{3,2,1,0:T(8,128)} fusion(f32[6,4,32,256]{3,2,1,0:T(8,128)S(1)} %fusion.7, f32[256,64]{1,0:T(8,128)S(1)} %get-tuple-element.26, f32[256,64]{1,0:T(8,128)S(1)} %get-tuple-element.25), kind=kOutput, calls=%fused_computation.112 | convolution fusion | flops 302022656 | bytes 1310720 | tf_op jit(solution)/shard_map/vizt,tk->vizk/dot_general | solution.py:155
  107.0 31.6 %all-reduce.2.cloned.1.call-done = f32[6,4,32,128]{3,2,1,0:T(8,128)} async-done(((f32[6,4,32,128]{3,2,1,0:T(8,128)}), f32[6,4,32,128]{3,2,1,0:T(8,128)}) %all-reduce.2.cloned.1.call-update) | async-done | bytes 393232 | tf_op jit(solution)/shard_map/psum | solution.py:158
  138.6 2.7 %convolution_select_fusion = f32[6,4,32,256]{3,2,1,0:T(8,128)} fusion(f32[6,4,32,256]{3,2,1,0:T(8,128)S(1)} %fusion.7, f32[6,4,32,128]{3,2,1,0:T(8,128)} %all-reduce.2.cloned.1.call-done, pred[]{:T(512)S(6)} %eq.25, f32[4,128]{1,0:T(4,128)S(1)} %pad_maximum_fusion.8, f32[256,64]{1,0:T(8,128)S(1)} %get-tuple-element.26, f32[256,64]{1,0:T(8,128)S(1)} %get-tuple-element.25), kind=kOutput, calls=%fused_computation.9 | convolution fusion | flops 302317568 | bytes 2099201 | tf_op jit(solution)/shard_map/vizk,tk->vizt/dot_general | solution.py:160
  (46 shorter events, 0.8 us)
Async XLA Ops:
  6.5 1.5 copy-start
  6.5 132.1 %all-reduce.2.cloned.1.call-start = ((), (), s32[]{:S(2)}) async-start(), calls=%async_computation | async-start | bytes 786432 | tf_op jit(solution)/shard_map/psum | solution.py:158
  9.2 19.5 %collective-permute-start.2 = (f32[7,3,32,256]{3,2,1,0:T(8,128)}, f32[7,3,32,256]{3,2,1,0:T(8,128)S(1)}, u32[]{:S(2)}, u32[]{:S(2)}) collective-permute-start(f32[7,3,32,256]{3,2,1,0:T(8,128)} %get-tuple-element.24), channel_id=1, source_target_pairs={{16,0},{0,16},{17,1},{1,17},{18,2},{2,18},{19,3},{3,19},{20,4},{4,... | collective-permute-start | bytes 2064392 | tf_op jit(solution)/shard_map/ppermute | solution.py:32
  12.2 30.4 %collective-permute-start = (f32[7,3,32,256]{3,2,1,0:T(8,128)}, f32[7,3,32,256]{3,2,1,0:T(8,128)}, u32[]{:S(2)}, u32[]{:S(2)}) collective-permute-start(f32[7,3,32,256]{3,2,1,0:T(8,128)} %get-tuple-element.24), channel_id=1, source_target_pairs={{0,8},{4,12},{8,0},{12,4},{1,9},{5,13},{9,1},{13,5},{2,10},{6,14},... | collective-permute-start | bytes 2064392 | tf_op jit(solution)/shard_map/ppermute | solution.py:20
  13.7 28.9 %collective-permute-start.1 = (f32[7,3,32,256]{3,2,1,0:T(8,128)}, f32[7,3,32,256]{3,2,1,0:T(8,128)S(1)}, u32[]{:S(2)}, u32[]{:S(2)}) collective-permute-start(f32[7,3,32,256]{3,2,1,0:T(8,128)} %get-tuple-element.23), channel_id=1, source_target_pairs={{0,16},{16,0},{1,17},{17,1},{2,18},{18,2},{3,19},{19,3},{4,20},{20... | collective-permute-start | bytes 2064392 | tf_op jit(solution)/shard_map/ppermute | solution.py:30
  14.4 28.2 %copy-start.10 = (f32[7]{0:T(128)S(1)}, f32[7]{0:T(128)}, u32[]{:S(2)}) copy-start(f32[7]{0:T(128)} %constant.69.clone) | copy-start | bytes 88
  14.4 29.7 %copy-start.7 = (f32[6,4,32,256]{3,2,1,0:T(8,128)}, f32[6,4,32,256]{3,2,1,0:T(8,128)S(1)}, u32[]{:S(2)}) copy-start(f32[6,4,32,256]{3,2,1,0:T(8,128)S(1)} %broadcast_dynamic-update-slice_fusion) | copy-start | bytes 2359300
  28.7 15.4 %copy-start.3 = (f32[7,3,32,256]{3,2,1,0:T(8,128)}, f32[7,3,32,256]{3,2,1,0:T(8,128)S(1)}, u32[]{:S(2)}) copy-start(f32[7,3,32,256]{3,2,1,0:T(8,128)S(1)} %collective-permute-done.2) | copy-start | bytes 2064388
  42.6 3.5 %copy-start.1 = (f32[7,3,32,256]{3,2,1,0:T(8,128)}, f32[7,3,32,256]{3,2,1,0:T(8,128)S(1)}, u32[]{:S(2)}) copy-start(f32[7,3,32,256]{3,2,1,0:T(8,128)S(1)} %collective-permute-done.1) | copy-start | bytes 2064388
  47.9 5.6 %copy-start.5 = (f32[7,10,32,256]{3,2,1,0:T(8,128)S(1)}, f32[7,10,32,256]{3,2,1,0:T(8,128)}, u32[]{:S(2)}) copy-start(f32[7,10,32,256]{3,2,1,0:T(8,128)} %get-tuple-element.21) | copy-start | bytes 6881284
  50.5 9.2 %collective-permute-start.4 = (f32[7,10,32,3]{2,0,3,1:T(8,128)}, f32[7,10,32,3]{2,0,3,1:T(8,128)}, u32[]{:S(2)}, u32[]{:S(2)}) collective-permute-start(f32[7,10,32,3]{2,0,3,1:T(8,128)} %copy.7), channel_id=1, source_target_pairs={{4,0},{8,4},{12,8},{0,12},{5,1},{9,5},{13,9},{1,13},{6,2},{10,6},{... | collective-permute-start | bytes 80648 | tf_op jit(solution)/shard_map/ppermute | solution.py:32
  53.2 7.9 %collective-permute-start.3 = (f32[7,10,32,3]{2,0,3,1:T(8,128)}, f32[7,10,32,3]{2,0,3,1:T(8,128)}, u32[]{:S(2)}, u32[]{:S(2)}) collective-permute-start(f32[7,10,32,3]{2,0,3,1:T(8,128)} %copy.6), channel_id=1, source_target_pairs={{0,4},{4,8},{8,12},{12,0},{1,5},{5,9},{9,13},{13,1},{2,6},{6,10},{... | collective-permute-start | bytes 80648 | tf_op jit(solution)/shard_map/ppermute | solution.py:30
  65.0 1.1 copy-start.2
  65.1 1.3 copy-start.4
  68.3 14.1 %collective-permute-start.6 = (f32[7,10,3,262]{3,2,1,0:T(4,128)S(1)}, f32[7,10,3,262]{3,2,1,0:T(4,128)S(1)}, u32[]{:S(2)}, u32[]{:S(2)}) collective-permute-start(f32[7,10,3,262]{3,2,1,0:T(4,128)S(1)} %get-tuple-element.18), channel_id=1, source_target_pairs={{1,0},{2,1},{3,2},{0,3},{5,4},{6,5},{7,6},{4,7},{9,8},{10,9},{11,1... | collective-permute-start | bytes 660248 | tf_op jit(solution)/shard_map/ppermute | solution.py:32
  72.2 20.3 %collective-permute-start.5 = (f32[7,10,3,262]{3,2,1,0:T(4,128)S(1)}, f32[7,10,3,262]{3,2,1,0:T(4,128)S(1)}, u32[]{:S(2)}, u32[]{:S(2)}) collective-permute-start(f32[7,10,3,262]{3,2,1,0:T(4,128)S(1)} %get-tuple-element.17), channel_id=1, source_target_pairs={{0,1},{1,2},{2,3},{3,0},{4,5},{5,6},{6,7},{7,4},{8,9},{9,10},{10,1... | collective-permute-start | bytes 660248 | tf_op jit(solution)/shard_map/ppermute | solution.py:30
  99.4 5.0 %copy-start.6 = (f32[6,5,32,256]{3,2,1,0:T(8,128)S(1)}, f32[6,5,32,256]{3,2,1,0:T(8,128)}, u32[]{:S(2)}) copy-start(f32[6,5,32,256]{3,2,1,0:T(8,128)} %add_multiply_fusion.3) | copy-start | bytes 2949124
  99.4 5.0 %copy-start.8 = (f32[6,4,32,256]{3,2,1,0:T(8,128)S(1)}, f32[6,4,32,256]{3,2,1,0:T(8,128)}, u32[]{:S(2)}) copy-start(f32[6,4,32,256]{3,2,1,0:T(8,128)} %copy-done.7) | copy-start | bytes 2359300
  99.4 5.0 %copy-start.9 = (f32[6,4,32,256]{3,2,1,0:T(8,128)S(1)}, f32[6,4,32,256]{3,2,1,0:T(8,128)}, u32[]{:S(2)}) copy-start(f32[6,4,32,256]{3,2,1,0:T(8,128)} %param.5) | copy-start | bytes 2359300
  105.2 1.6 %copy-start.11 = (s32[4]{0:T(128)S(1)}, s32[4]{0:T(128)}, u32[]{:S(2)}) copy-start(s32[4]{0:T(128)} %param.8) | copy-start | bytes 52
Sparse Core Ops, SparseCore 0:
  106.9 31.6 all-reduce.1
where the time goes:
time: 149 us; the launch traced here: 148 us
  waiting for transfers between devices  73.5 us (49%)
  other arithmetic  36.1 us (24%)
  between operations  13.8 us (9%)
  local copies, waits for them, and re-layouts  11 us (7%)
  starting transfers between devices  9.39 us (6%)
  matrix products  4.34 us (3%)
    psum x1, waiting for transfers between devices, apply_filter(): coefficients = lax.psum(coefficients, 'theta')  31.6 us
    ppermute x3, waiting for transfers between devices, with_halo(): lax.ppermute(tail, axis, [(i, (i + 1) % count) for i in range(count)])  23.9 us
    ppermute x3, waiting for transfers between devices, with_halo(): lax.ppermute(head, axis, [((i + 1) % count, i) for i in range(count)])  18 us
    add x2, other arithmetic, face_fluxes(): return upwind_part + downwind_part  10.9 us
    concatenate x2, other arithmetic, with_halo(): jnp.concatenate([lax.ppermute(tail, axis, [(i, (i + 1) % count) for i in...  8.27 us
    ppermute x3, starting transfers between devices, with_halo(): lax.ppermute(head, axis, [((i + 1) % count, i) for i in range(count)])  7.17 us
    mul x1, other arithmetic, tendency(): weighted = face_radius * radial_flux  5.18 us
    slice x3, local copies, waits for them, and re-layouts, with_halo(): lax.slice_in_dim(cells, cells.shape[dim] - width, cells.shape[dim], axis=...  4.38 us
  transfers between devices with their start and end apart: 8, of which 5 were waited for; matrix products, arithmetic and copies ran while one was open for 11% of the time, Pallas kernels for 0%

commit v1 on v0

--- a/solution.py
+++ b/solution.py
@@ -12,6 +12,15 @@
 liquid_ratio = 4.4
 gas_ratio = 1.4
 liquid_stiffness = 0.6
+
+
+def sum_by_hops(block, axis):
+    n_dev = lax.axis_size(axis)
+    total, stride = (block, 1)
+    while stride < n_dev:
+        total = total + lax.ppermute(total, axis, [(i, i ^ stride) for i in range(n_dev)])
+        stride = 2 * stride
+    return total
 
 
 def passed_along(value, axis, steps):
@@ -155,7 +164,7 @@
     coefficients = jnp.einsum(
         "vizt,tk->vizk", cycle_block, fourier_table, precision=lax.Precision.HIGHEST
     )
-    coefficients = lax.psum(coefficients, "theta")
+    coefficients = sum_by_hops(coefficients, "theta")
     coefficients = coefficients * weights[None, :, None, :]
     return jnp.einsum("vizk,tk->vizt", coefficients, fourier_table, precision=lax.Precision.HIGHEST)
 

time: 149 us -> 115 us (0.77)
  waiting for transfers between devices: 73.5 us -> 53.6 us
  between operations: 13.8 us -> 0.39 us
  matrix products: 4.34 us -> 2.6 us
    psum x1 -> x0, waiting for transfers between devices: 31.6 us -> none  [apply_filter(): coefficients = lax.psum(coefficients, 'theta')]
    ppermute x0 -> x2, waiting for transfers between devices: none -> 11.7 us  [sum_by_hops(): lax.ppermute(total, axis, [(i, i ^ stride) for i in range(n_dev)])]
  transfers between devices with their start and end apart: 8 -> 9, of which waited for: 5 -> 6; matrix products, arithmetic and copies ran while one was open for 11% -> 15% of each run, Pallas kernels for 0% -> 0%
where the time goes in v1:
time: 115 us; the launch traced here: 114 us
  waiting for transfers between devices  53.6 us (47%)
  other arithmetic  36.2 us (31%)
  local copies, waits for them, and re-layouts  11 us (10%)
  starting transfers between devices  10.5 us (9%)
  matrix products  2.6 us (2%)
    ppermute x3, waiting for transfers between devices, with_halo(): lax.ppermute(tail, axis, [(i, (i + 1) % count) for i in range(count)])  23.9 us
    ppermute x3, waiting for transfers between devices, with_halo(): lax.ppermute(head, axis, [((i + 1) % count, i) for i in range(count)])  18 us
    ppermute x2, waiting for transfers between devices, sum_by_hops(): lax.ppermute(total, axis, [(i, i ^ stride) for i in range(n_dev)])  11.7 us
    add x2, other arithmetic, face_fluxes(): return upwind_part + downwind_part  10.9 us
    concatenate x2, other arithmetic, with_halo(): jnp.concatenate([lax.ppermute(tail, axis, [(i, (i + 1) % count) for i in...  8.27 us
    ppermute x3, starting transfers between devices, with_halo(): lax.ppermute(head, axis, [((i + 1) % count, i) for i in range(count)])  7.17 us
    mul x1, other arithmetic, tendency(): weighted = face_radius * radial_flux  5.2 us
    slice x3, local copies, waits for them, and re-layouts, with_halo(): lax.slice_in_dim(cells, cells.shape[dim] - width, cells.shape[dim], axis=...  4.38 us
  transfers between devices with their start and end apart: 9, of which 6 were waited for; matrix products, arithmetic and copies ran while one was open for 15% of the time, Pallas kernels for 0%

profile of v1, /device:TPU:0, one launch (start us, length us, event | category | flops | bytes accessed | tf_op | source)
XLA Modules:
  0.0 114.3 jit_solution(14251777406659594989)
XLA Ops:
  0.0 1.4 %bitcast_dynamic-update-slice_fusion = (f32[6,4,32,256]{3,2,1,0:T(8,128)S(1)}, f32[4,32,256]{2,1,0:T(8,128)S(1)}) fusion(f32[6,4,32,256]{3,2,1,0:T(8,128)S(1)} %broadcast_dynamic-update-slice_fusion.1, f32[6,4,32,256]{3,2,1,0:T(8,128)} %param.6, f32[4]{0:T(128)S(1)} %get-tuple-element.28, s32[4,32,256]{2,1,0:T(8,128)} %param.7), kind=kLoop, calls=%fused_computation.97 | loop fusion | flops 622592 | bytes 1049088
  1.5 1.2 %fusion.11 = (f32[7,3,32,256]{3,2,1,0:T(8,128)}, f32[7,3,32,256]{3,2,1,0:T(8,128)}) fusion(f32[6,4,32,256]{3,2,1,0:T(8,128)S(1)} %copy-done, f32[1,4,32,256]{3,2,1,0:T(8,128)S(1)} %bitcast.47), kind=kLoop, calls=%fused_computation.35 | loop fusion | flops 344064 | bytes 2293760 | tf_op jit(solution)/shard_map/concatenate | solution.py:180
  2.7 3.0 %collective-permute-start.2 = (f32[7,3,32,256]{3,2,1,0:T(8,128)}, f32[7,3,32,256]{3,2,1,0:T(8,128)S(1)}, u32[]{:S(2)}, u32[]{:S(2)}) collective-permute-start(f32[7,3,32,256]{3,2,1,0:T(8,128)} %get-tuple-element.24), channel_id=1, source_target_pairs={{16,0},{0,16},{17,1},{1,17},{18,2},{2,18},{19,3},{3,19},{20,4},{4,... | collective-permute-start | bytes 2064392 | tf_op jit(solution)/shard_map/ppermute | solution.py:41
  5.7 1.5 %collective-permute-start = (f32[7,3,32,256]{3,2,1,0:T(8,128)}, f32[7,3,32,256]{3,2,1,0:T(8,128)}, u32[]{:S(2)}, u32[]{:S(2)}) collective-permute-start(f32[7,3,32,256]{3,2,1,0:T(8,128)} %get-tuple-element.24), channel_id=1, source_target_pairs={{0,8},{4,12},{8,0},{12,4},{1,9},{5,13},{9,1},{13,5},{2,10},{6,14},... | collective-permute-start | bytes 2064392 | tf_op jit(solution)/shard_map/ppermute | solution.py:29
  7.2 0.5 collective-permute-start.1
  7.9 0.6 fusion.48
  8.5 13.7 %collective-permute-done.2 = f32[7,3,32,256]{3,2,1,0:T(8,128)S(1)} collective-permute-done((f32[7,3,32,256]{3,2,1,0:T(8,128)}, f32[7,3,32,256]{3,2,1,0:T(8,128)S(1)}, u32[]{:S(2)}, u32[]{:S(2)}) %collective-permute-start.2) | collective-permute-done | bytes 688160 | tf_op jit(solution)/shard_map/ppermute | solution.py:41
  22.3 13.8 %collective-permute-done.1 = f32[7,3,32,256]{3,2,1,0:T(8,128)S(1)} collective-permute-done((f32[7,3,32,256]{3,2,1,0:T(8,128)}, f32[7,3,32,256]{3,2,1,0:T(8,128)S(1)}, u32[]{:S(2)}, u32[]{:S(2)}) %collective-permute-start.1) | collective-permute-done | bytes 688160 | tf_op jit(solution)/shard_map/ppermute | solution.py:39
  36.1 1.5 %multiply_select_fusion = f32[7,3,32,256]{3,2,1,0:T(8,128)S(1)} fusion(f32[7,3,32,256]{3,2,1,0:T(8,128)S(1)} %collective-permute-done.1, f32[7,3,32,256]{3,2,1,0:T(8,128)} %collective-permute-done, f32[7]{0:T(128)S(1)} %copy-done.10, pred[]{:T(512)S(6)} %eq.25), kind=kLoop, calls=%fused_computation.37 | loop fusion | flops 344064 | bytes 2064413 | tf_op jit(solution)/shard_map/jit(_where)/select_n | solution.py:188
  37.6 1.9 %pad_maximum_fusion.2 = (f32[7,10,32,256]{3,2,1,0:T(8,128)}, f32[7,10,32,256]{3,2,1,0:T(8,128)S(1)}) fusion(f32[7,3,32,256]{3,2,1,0:T(8,128)S(1)} %broadcast_select_fusion, f32[1,4,32,256]{3,2,1,0:T(8,128)S(1)} %bitcast.49, f32[6,4,32,256]{3,2,1,0:T(8,128)S(1)} %copy-done, f32[7,3,32,256]{3,2,1,0:T(8,128)S(1)} %multiply_select_fusion, ...), kind=kLoop, calls=%fused_computation.2 | loop fusion | flops 2867200 | bytes 8257536 | tf_op jit(solution)/shard_map/concatenate | solution.py:190
  39.6 1.8 %fusion.57 = (f32[7,10,32,3]{3,2,1,0:T(8,128)}, f32[7,10,32,3]{3,2,1,0:T(8,128)}) fusion(f32[7,10,32,256]{3,2,1,0:T(8,128)S(1)} %get-tuple-element.22), kind=kLoop, calls=%fused_computation.128 | loop fusion | bytes 107520 | tf_op jit(solution)/shard_map/slice | solution.py:36
  41.3 2.6 %copy.7 = f32[7,10,32,3]{2,0,3,1:T(8,128)} copy(f32[7,10,32,3]{3,2,1,0:T(8,128)} %get-tuple-element.20) | data formatting | bytes 53760 | tf_op jit(solution)/shard_map/slice | solution.py:35
  43.9 0.3 collective-permute-start.4
  44.2 2.5 %copy.6 = f32[7,10,32,3]{2,0,3,1:T(8,128)} copy(f32[7,10,32,3]{3,2,1,0:T(8,128)} %get-tuple-element.19) | data formatting | bytes 53760 | tf_op jit(solution)/shard_map/slice | solution.py:36
  46.7 0.2 collective-permute-start.3
  47.3 0.7 add_multiply_fusion
  48.0 5.2 %add_multiply_fusion.3 = f32[6,5,32,256]{3,2,1,0:T(8,128)} fusion(f32[6,10,32,256]{3,2,1,0:T(8,128)S(1)} %get-tuple-element.16, f32[6,10,32,256]{3,2,1,0:T(8,128)S(1)} %get-tuple-element.15, f32[5]{0:T(128)S(1)} %add_convert_fusion), kind=kLoop, calls=%fused_computation.20 | loop fusion | flops 31948800 | bytes 10813460 | tf_op jit(solution)/shard_map/mul | solution.py:123
  53.2 1.4 %copy.9 = f32[7,10,32,3]{3,2,1,0:T(8,128)S(1)} copy(f32[7,10,32,3]{2,0,3,1:T(8,128)} %collective-permute-done.4) | data formatting | bytes 53760 | tf_op jit(solution)/shard_map/ppermute | solution.py:41
  54.6 1.4 %copy.8 = f32[7,10,32,3]{3,2,1,0:T(8,128)S(1)} copy(f32[7,10,32,3]{2,0,3,1:T(8,128)} %collective-permute-done.3) | data formatting | bytes 53760 | tf_op jit(solution)/shard_map/ppermute | solution.py:39
  56.0 2.6 %pad_maximum_fusion.1 = f32[7,10,32,262]{3,2,1,0:T(8,128)S(1)} fusion(f32[7,10,32,3]{3,2,1,0:T(8,128)S(1)} %copy.9, f32[7,3,32,256]{3,2,1,0:T(8,128)} %copy-done.3, f32[1,4,32,256]{3,2,1,0:T(8,128)S(1)} %bitcast.50, f32[6,4,32,256]{3,2,1,0:T(8,128)S(1)} %copy-done, f32[7,3,32,256]{3,2,1,0:T(8,128)} %copy-done.1, f32[7,10,32,3]{3,2,1,0:T(8,128)S(1)} %copy.8), kind=kLoop, calls=%fused_computation.1 | loop fusion | flops 2934400 | bytes 4695040 | tf_op jit(solution)/shard_map/concatenate | solution.py:37
  58.5 0.2 fusion.56
  58.7 0.9 copy-done.2
  59.6 0.2 copy-done.4
  59.8 0.2 multiply_dynamic-update-slice_fusion.1
  60.0 0.3 fusion.27
  60.3 0.3 fusion.26
  60.6 0.3 fusion.24
  60.9 0.3 fusion.23
  61.2 0.3 fusion.21
  61.5 0.3 add_multiply_fusion.1
  61.8 3.9 %collective-permute-start.6 = (f32[7,10,3,262]{3,2,1,0:T(4,128)S(1)}, f32[7,10,3,262]{3,2,1,0:T(4,128)S(1)}, u32[]{:S(2)}, u32[]{:S(2)}) collective-permute-start(f32[7,10,3,262]{3,2,1,0:T(4,128)S(1)} %get-tuple-element.18), channel_id=1, source_target_pairs={{1,0},{2,1},{3,2},{0,3},{5,4},{6,5},{7,6},{4,7},{9,8},{10,9},{11,1... | collective-permute-start | bytes 660248 | tf_op jit(solution)/shard_map/ppermute | solution.py:41
  65.7 5.9 %divide_add_fusion = f32[6,4,32,257]{3,2,1,0:T(8,128)S(1)} fusion(f32[6,4,32,262]{3,2,1,0:T(8,128)S(1)} %get-tuple-element.14, f32[6,4,32,262]{3,2,1,0:T(8,128)S(1)} %get-tuple-element.13), kind=kLoop, calls=%fused_computation.13 | loop fusion | flops 25461504 | bytes 8684544 | tf_op jit(solution)/shard_map/add | solution.py:112
  71.6 4.3 %collective-permute-done.6 = f32[7,10,3,262]{3,2,1,0:T(4,128)S(1)} collective-permute-done((f32[7,10,3,262]{3,2,1,0:T(4,128)S(1)}, f32[7,10,3,262]{3,2,1,0:T(4,128)S(1)}, u32[]{:S(2)}, u32[]{:S(2)}) %collective-permute-start.6) | collective-permute-done | bytes 220112 | tf_op jit(solution)/shard_map/ppermute | solution.py:41
  75.9 10.1 %collective-permute-done.5 = f32[7,10,3,262]{3,2,1,0:T(4,128)S(1)} collective-permute-done((f32[7,10,3,262]{3,2,1,0:T(4,128)S(1)}, f32[7,10,3,262]{3,2,1,0:T(4,128)S(1)}, u32[]{:S(2)}, u32[]{:S(2)}) %collective-permute-start.5) | collective-permute-done | bytes 220112 | tf_op jit(solution)/shard_map/ppermute | solution.py:39
  86.0 5.7 %pad_maximum_fusion = f32[7,10,38,262]{3,2,1,0:T(8,128)S(1)} fusion(f32[7,10,3,262]{3,2,1,0:T(4,128)S(1)} %collective-permute-done.6, f32[7,10,32,3]{3,2,1,0:T(8,128)S(1)} %copy.9, f32[7,3,32,256]{3,2,1,0:T(8,128)S(1)} %copy-done.4, f32[1,4,32,256]{3,2,1,0:T(8,128)S(1)} %bitcast.57, f32[6,4,32,256]{3,2,1,0:T(8,128)S(1)} %copy-done, ...), kind=kLoop, calls=%fused_computation | loop fusion | flops 4878440 | bytes 5575360 | tf_op jit(solution)/shard_map/concatenate | solution.py:37
  91.7 0.2 multiply_dynamic-update-slice_fusion.2
  91.9 0.1 fusion.33
  92.1 0.2 add_dynamic-update-slice_fusion.1
  92.3 0.2 fusion.31
  92.5 0.3 add_multiply_fusion.2
  92.9 5.0 %divide_add_fusion.1 = f32[6,4,33,256]{3,2,1,0:T(8,128)S(1)} fusion(f32[6,4,38,256]{3,2,1,0:T(8,128)S(1)} %get-tuple-element.12, f32[6,4,38,256]{3,2,1,0:T(8,128)S(1)} %get-tuple-element.11), kind=kLoop, calls=%fused_computation.17 | loop fusion | flops 26155008 | bytes 8921088 | tf_op jit(solution)/shard_map/add | solution.py:112
  97.9 0.7 fusion.7
  98.7 0.9 fusion.49
  99.5 0.2 collective-permute-start.7
  99.7 1.6 %collective-permute-done.7 = f32[6,4,32,128]{3,2,1,0:T(8,128)S(1)} collective-permute-done((f32[6,4,32,128]{3,2,1,0:T(8,128)S(1)}, f32[6,4,32,128]{3,2,1,0:T(8,128)S(1)}, u32[]{:S(2)}, u32[]{:S(2)}) %collective-permute-start.7) | collective-permute-done | bytes 393248 | tf_op jit(solution)/shard_map/ppermute | solution.py:21
  101.4 0.9 collective-permute-start.8
  102.5 10.1 %collective-permute-done.8 = f32[6,4,32,128]{3,2,1,0:T(8,128)S(1)} collective-permute-done((f32[6,4,32,128]{3,2,1,0:T(8,128)S(1)}, f32[6,4,32,128]{3,2,1,0:T(8,128)S(1)}, u32[]{:S(2)}, u32[]{:S(2)}) %collective-permute-start.8) | collective-permute-done | bytes 393248 | tf_op jit(solution)/shard_map/ppermute | solution.py:21
  112.6 1.7 %convolution_select_fusion = f32[6,4,32,256]{3,2,1,0:T(8,128)} fusion(f32[6,4,32,256]{3,2,1,0:T(8,128)S(1)} %fusion.7, f32[6,4,32,128]{3,2,1,0:T(8,128)S(1)} %add.582, f32[6,4,32,128]{3,2,1,0:T(8,128)S(1)} %collective-permute-done.8, pred[]{:T(512)S(6)} %eq.25, f32[4,128]{1,0:T(4,128)S(1)} %pad_maximum_fusion.8, f32[256,64]{1,0:T(8,128)S(1)} %get-tuple-element.26, ...), kind=kOutput, calls=%fused_computation.9 | convolution fusion | flops 302415872 | bytes 2492417 | tf_op jit(solution)/shard_map/vizk,tk->vizt/dot_general | solution.py:169
  (48 shorter events, 1.1 us)
Async XLA Ops:
  0.0 1.5 %copy-start = (f32[6,4,32,256]{3,2,1,0:T(8,128)S(1)}, f32[6,4,32,256]{3,2,1,0:T(8,128)}, u32[]{:S(2)}) copy-start(f32[6,4,32,256]{3,2,1,0:T(8,128)} %param.6) | copy-start | bytes 2359300
  2.7 19.5 %collective-permute-start.2 = (f32[7,3,32,256]{3,2,1,0:T(8,128)}, f32[7,3,32,256]{3,2,1,0:T(8,128)S(1)}, u32[]{:S(2)}, u32[]{:S(2)}) collective-permute-start(f32[7,3,32,256]{3,2,1,0:T(8,128)} %get-tuple-element.24), channel_id=1, source_target_pairs={{16,0},{0,16},{17,1},{1,17},{18,2},{2,18},{19,3},{3,19},{20,4},{4,... | collective-permute-start | bytes 2064392 | tf_op jit(solution)/shard_map/ppermute | solution.py:41
  5.7 30.4 %collective-permute-start = (f32[7,3,32,256]{3,2,1,0:T(8,128)}, f32[7,3,32,256]{3,2,1,0:T(8,128)}, u32[]{:S(2)}, u32[]{:S(2)}) collective-permute-start(f32[7,3,32,256]{3,2,1,0:T(8,128)} %get-tuple-element.24), channel_id=1, source_target_pairs={{0,8},{4,12},{8,0},{12,4},{1,9},{5,13},{9,1},{13,5},{2,10},{6,14},... | collective-permute-start | bytes 2064392 | tf_op jit(solution)/shard_map/ppermute | solution.py:29
  7.2 28.9 %collective-permute-start.1 = (f32[7,3,32,256]{3,2,1,0:T(8,128)}, f32[7,3,32,256]{3,2,1,0:T(8,128)S(1)}, u32[]{:S(2)}, u32[]{:S(2)}) collective-permute-start(f32[7,3,32,256]{3,2,1,0:T(8,128)} %get-tuple-element.23), channel_id=1, source_target_pairs={{0,16},{16,0},{1,17},{17,1},{2,18},{18,2},{3,19},{19,3},{4,20},{20... | collective-permute-start | bytes 2064392 | tf_op jit(solution)/shard_map/ppermute | solution.py:39
  7.8 28.3 %copy-start.10 = (f32[7]{0:T(128)S(1)}, f32[7]{0:T(128)}, u32[]{:S(2)}) copy-start(f32[7]{0:T(128)} %constant.69.clone) | copy-start | bytes 88
  7.9 29.7 %copy-start.7 = (f32[6,4,32,256]{3,2,1,0:T(8,128)}, f32[6,4,32,256]{3,2,1,0:T(8,128)S(1)}, u32[]{:S(2)}) copy-start(f32[6,4,32,256]{3,2,1,0:T(8,128)S(1)} %broadcast_dynamic-update-slice_fusion) | copy-start | bytes 2359300
  22.2 15.4 %copy-start.3 = (f32[7,3,32,256]{3,2,1,0:T(8,128)}, f32[7,3,32,256]{3,2,1,0:T(8,128)S(1)}, u32[]{:S(2)}) copy-start(f32[7,3,32,256]{3,2,1,0:T(8,128)S(1)} %collective-permute-done.2) | copy-start | bytes 2064388
  36.1 3.5 %copy-start.1 = (f32[7,3,32,256]{3,2,1,0:T(8,128)}, f32[7,3,32,256]{3,2,1,0:T(8,128)S(1)}, u32[]{:S(2)}) copy-start(f32[7,3,32,256]{3,2,1,0:T(8,128)S(1)} %collective-permute-done.1) | copy-start | bytes 2064388
  41.3 5.6 %copy-start.5 = (f32[7,10,32,256]{3,2,1,0:T(8,128)S(1)}, f32[7,10,32,256]{3,2,1,0:T(8,128)}, u32[]{:S(2)}) copy-start(f32[7,10,32,256]{3,2,1,0:T(8,128)} %get-tuple-element.21) | copy-start | bytes 6881284
  43.9 9.3 %collective-permute-start.4 = (f32[7,10,32,3]{2,0,3,1:T(8,128)}, f32[7,10,32,3]{2,0,3,1:T(8,128)}, u32[]{:S(2)}, u32[]{:S(2)}) collective-permute-start(f32[7,10,32,3]{2,0,3,1:T(8,128)} %copy.7), channel_id=1, source_target_pairs={{4,0},{8,4},{12,8},{0,12},{5,1},{9,5},{13,9},{1,13},{6,2},{10,6},{... | collective-permute-start | bytes 80648 | tf_op jit(solution)/shard_map/ppermute | solution.py:41
  46.7 7.9 %collective-permute-start.3 = (f32[7,10,32,3]{2,0,3,1:T(8,128)}, f32[7,10,32,3]{2,0,3,1:T(8,128)}, u32[]{:S(2)}, u32[]{:S(2)}) collective-permute-start(f32[7,10,32,3]{2,0,3,1:T(8,128)} %copy.6), channel_id=1, source_target_pairs={{0,4},{4,8},{8,12},{12,0},{1,5},{5,9},{9,13},{13,1},{2,6},{6,10},{... | collective-permute-start | bytes 80648 | tf_op jit(solution)/shard_map/ppermute | solution.py:39
  58.5 1.1 copy-start.2
  58.5 1.3 %copy-start.4 = (f32[7,3,32,256]{3,2,1,0:T(8,128)S(1)}, f32[7,3,32,256]{3,2,1,0:T(8,128)}, u32[]{:S(2)}) copy-start(f32[7,3,32,256]{3,2,1,0:T(8,128)} %copy-done.3) | copy-start | bytes 2064388
  61.8 14.1 %collective-permute-start.6 = (f32[7,10,3,262]{3,2,1,0:T(4,128)S(1)}, f32[7,10,3,262]{3,2,1,0:T(4,128)S(1)}, u32[]{:S(2)}, u32[]{:S(2)}) collective-permute-start(f32[7,10,3,262]{3,2,1,0:T(4,128)S(1)} %get-tuple-element.18), channel_id=1, source_target_pairs={{1,0},{2,1},{3,2},{0,3},{5,4},{6,5},{7,6},{4,7},{9,8},{10,9},{11,1... | collective-permute-start | bytes 660248 | tf_op jit(solution)/shard_map/ppermute | solution.py:41
  65.7 20.3 %collective-permute-start.5 = (f32[7,10,3,262]{3,2,1,0:T(4,128)S(1)}, f32[7,10,3,262]{3,2,1,0:T(4,128)S(1)}, u32[]{:S(2)}, u32[]{:S(2)}) collective-permute-start(f32[7,10,3,262]{3,2,1,0:T(4,128)S(1)} %get-tuple-element.17), channel_id=1, source_target_pairs={{0,1},{1,2},{2,3},{3,0},{4,5},{5,6},{6,7},{7,4},{8,9},{9,10},{10,1... | collective-permute-start | bytes 660248 | tf_op jit(solution)/shard_map/ppermute | solution.py:39
  92.9 5.0 %copy-start.6 = (f32[6,5,32,256]{3,2,1,0:T(8,128)S(1)}, f32[6,5,32,256]{3,2,1,0:T(8,128)}, u32[]{:S(2)}) copy-start(f32[6,5,32,256]{3,2,1,0:T(8,128)} %add_multiply_fusion.3) | copy-start | bytes 2949124
  92.9 5.0 %copy-start.8 = (f32[6,4,32,256]{3,2,1,0:T(8,128)S(1)}, f32[6,4,32,256]{3,2,1,0:T(8,128)}, u32[]{:S(2)}) copy-start(f32[6,4,32,256]{3,2,1,0:T(8,128)} %copy-done.7) | copy-start | bytes 2359300
  92.9 5.0 %copy-start.9 = (f32[6,4,32,256]{3,2,1,0:T(8,128)S(1)}, f32[6,4,32,256]{3,2,1,0:T(8,128)}, u32[]{:S(2)}) copy-start(f32[6,4,32,256]{3,2,1,0:T(8,128)} %param.5) | copy-start | bytes 2359300
  98.7 3.7 %copy-start.11 = (s32[4]{0:T(128)S(1)}, s32[4]{0:T(128)}, u32[]{:S(2)}) copy-start(s32[4]{0:T(128)} %param.8) | copy-start | bytes 52
  99.5 1.8 %collective-permute-start.7 = (f32[6,4,32,128]{3,2,1,0:T(8,128)S(1)}, f32[6,4,32,128]{3,2,1,0:T(8,128)S(1)}, u32[]{:S(2)}, u32[]{:S(2)}) collective-permute-start(f32[6,4,32,128]{3,2,1,0:T(8,128)S(1)} %fusion.49), channel_id=1, source_target_pairs={{0,4},{4,0},{8,12},{12,8},{1,5},{5,1},{9,13},{13,9},{2,6},{6,2},{1... | collective-permute-start | bytes 1179656 | tf_op jit(solution)/shard_map/ppermute | solution.py:21
  101.4 11.2 %collective-permute-start.8 = (f32[6,4,32,128]{3,2,1,0:T(8,128)S(1)}, f32[6,4,32,128]{3,2,1,0:T(8,128)S(1)}, u32[]{:S(2)}, u32[]{:S(2)}) collective-permute-start(f32[6,4,32,128]{3,2,1,0:T(8,128)S(1)} %add.582), channel_id=1, source_target_pairs={{0,8},{4,12},{8,0},{12,4},{1,9},{5,13},{9,1},{13,5},{2,10},{6,14},... | collective-permute-start | bytes 1179656 | tf_op jit(solution)/shard_map/ppermute | solution.py:21
